TPU v7x, 128 devices: a whole 4x4x4 slice. The times are simulated.
128 devices in a mesh: gx: 8 (over z, core), gy: 16 (over x, y).
Axes of the slice: x: 4, y: 4, z: 4, core: 2. Of those that a mesh axis runs over, the one named last changes fastest.
Arguments:
- phase_box: bfloat16 [1024, 32, 1024], P(('gx', 'gy')), may hold values from 0 to 1
- matrix_density: float32 [256, 512, 128], P('gx', 'gy'), may hold values from 0.1 to 1
- box_corner: int32 [3, 1024], P(None, ('gx', 'gy')), may hold values from 0 to 480, as said below
Outputs:
- phase_next: bfloat16 [1024, 32, 1024], P(('gx', 'gy'))
- matrix_next: float32 [256, 512, 128], P('gx', 'gy')
Inputs may be any that keep to these rules, and one draw needn't show every extreme that they name: Every box lies inside the grid. Cell c is kept by device c // 8 of gx+gy, whose gx index equals box_corner[0, c] // 32. Among the cells of one device at most 1 have the same box_corner[1] // 32, and in every draw each device has 1 such cells for some value.
All inputs are finite; a program needn't handle non-finite values.
Results may differ from a plain program's by a relative error of at most 0.0095.
Values may be sent and summed in bfloat16 or wider, within the bound.
A program may use at most 128 MiB of HBM per device.

v0:
```python
import jax
import jax.numpy as jnp
from jax import lax
from jax.experimental import pallas as pl
from jax.experimental.pallas import tpu as pltpu
from jax.sharding import PartitionSpec as P

B = 32
LANES = 128
GROUP = LANES // B
SIDE = 4

def signal(axis, target):
    pl.semaphore_signal(
        pltpu.get_barrier_semaphore(),
        inc=1,
        device_id={axis: target},
        device_id_type=pl.DeviceIdType.MESH,
    )


def remote(src, dst, send, recv, axis, target):
    return pltpu.make_async_remote_copy(
        src_ref=src,
        dst_ref=dst,
        send_sem=send,
        recv_sem=recv,
        device_id={axis: target},
        device_id_type=pl.DeviceIdType.MESH,
    )


def greet():
    me, row = lax.axis_index("gy"), lax.axis_index("gx")
    columns, rows = lax.axis_size("gy"), lax.axis_size("gx")
    high, low = me // SIDE, lax.rem(me, SIDE)
    count = 0
    for step in (1, SIDE - 1):
        signal("gy", lax.rem(high + step, SIDE) * SIDE + low)
        signal("gy", high * SIDE + lax.rem(low + step, SIDE))
        count += 2
    for axis, at, size, step in (("gx", row, rows, 1), ("gx", row, rows, -1)):
        there = (at < size - 1) if step > 0 else (at > 0)
        count += there.astype(jnp.int32)

        @pl.when(there)
        def _():
            signal(axis, at + step)

    for step in (1, -1):
        far = (low == (SIDE - 1 if step > 0 else 0)) & (
            (me < columns - 1) if step > 0 else (me > 0)
        )
        count += far.astype(jnp.int32)

        @pl.when(far)
        def _():
            signal("gy", me + step)

    return count


class Exchange:
    def __init__(self, src, dst, stage, relay, send, recv, own, share_y):
        self.src, self.dst, self.stage, self.relay = src, dst, stage, relay
        self.send, self.recv, self.own = send, recv, own
        me = lax.axis_index("gy")
        self.at = (me // SIDE, lax.rem(me, SIDE))
        self.share = (SIDE // 2, share_y)
        self.rows = src.shape[2] // 2

    def turn(self, axis, step):
        return lax.rem(self.at[axis] + SIDE + step, SIDE)

    def device(self, axis, step):
        other, moved = self.at[1 - axis], self.turn(axis, step)
        return moved * SIDE + other if axis == 0 else other * SIDE + moved

    def whole(self, ref, half, first, second):
        rest = pl.ds(half * self.rows, self.rows)
        return ref.at[first, second, rest]

    def block(self, half, stage, goal, part):
        if stage == 1:
            return self.stage.at[half, part, goal]
        return self.whole(self.src, half, *((goal, part) if half == 0 else (part, goal)))

    def place(self, half, stage, origin, part):
        if stage == 0:
            return self.stage.at[half, origin, part]
        return self.whole(self.dst, half, *((part, origin) if half == 0 else (origin, part)))

    def copies(self, half, stage):
        axis = (half + stage) % 2
        share = self.share[axis]
        parts = (pl.ds(0, share), pl.ds(share, SIDE - share))
        sizes = (share, SIDE - share)
        every = pl.ds(0, SIDE)
        out = []
        for kind in ("relay", "direct", "forward"):
            for side in range(2):
                step = 1 if side == 0 else -1
                if kind == "direct":
                    src = self.block(half, stage, self.turn(axis, step), every)
                    dst = self.place(half, stage, self.at[axis], every)
                else:
                    hold = self.relay.at[half, stage, side, pl.ds(0, sizes[side])]
                    if kind == "relay":
                        src, dst = self.block(half, stage, self.turn(axis, 2), parts[side]), hold
                    else:
                        src = hold
                        dst = self.place(half, stage, self.turn(axis, -step), parts[side])
                at = (half, stage, len(out))
                out.append(
                    remote(src, dst, self.send.at[at], self.recv.at[at], "gy", self.device(axis, step))
                )
        return out

    def prepare(self):
        x, y = self.at
        self.stage[0, x] = self.src[x, :, : self.rows]
        self.stage[1, y] = self.src[:, y, self.rows :]

    def start(self, stage, half):
        copies = self.copies(half, stage)
        for copy in copies[:4]:
            copy.start()
        if stage == 1:
            self.kept(half).start()

    def forward(self, stage, half):
        copies = self.copies(half, stage)
        for side in range(2):
            copies[side].wait_recv()
            copies[4 + side].start()

    def arrive(self, stage, half):
        for copy in self.copies(half, stage)[2:]:
            copy.wait_recv()

    def kept(self, half):
        axis = (half + 1) % 2
        every = pl.ds(0, SIDE)
        return pltpu.make_async_copy(
            self.block(half, 1, self.at[axis], every),
            self.place(half, 1, self.at[axis], every),
            self.own.at[half],
        )

    def finish(self):
        for half in range(2):
            for stage in range(2):
                for copy in self.copies(half, stage):
                    copy.wait_send()
            self.kept(half).wait()


def gather_kernel(
    source, phase, table, low, boxes, places, density,
    outbox, stage, relay, half, send, recv, table_send, table_recv,
    y_send, y_recv, x_send, x_recv, own,
):
    me, row = lax.axis_index("gy"), lax.axis_index("gx")
    columns, rows = lax.axis_size("gy"), lax.axis_size("gx")
    edge = low.shape[0]
    part = edge // 2
    barrier = pltpu.get_barrier_semaphore()
    others = [lax.rem(me + k, columns) for k in range(1, columns)]
    senders = [lax.rem(me + columns - k, columns) for k in range(1, columns)]
    for target in others:
        signal("gy", target)

    @pl.when(row > 0)
    def _():
        signal("gx", row - 1)

    @pl.when(row < rows - 1)
    def _():
        signal("gx", row + 1)

    def fill(s, carry):
        outbox[s // SIDE, lax.rem(s, SIDE)] = phase[source[s]]
        return carry

    lax.fori_loop(0, columns, fill, 0)

    @pl.when(me == columns - 1)
    def _():
        half[...] = jnp.zeros_like(half)

    boxes_out = Exchange(outbox, boxes, stage, relay, send, recv, own, 3)
    boxes_out.prepare()

    neighbours = (row > 0).astype(jnp.int32) + (row < rows - 1).astype(jnp.int32)
    pl.semaphore_wait(barrier, columns - 1 + neighbours)

    def along_y(k):
        rest = pl.ds(k * part, part)
        return remote(low.at[rest], half.at[rest], y_send.at[k], y_recv.at[k], "gy", me - 1)

    def along_x(k):
        src = low if k == 2 else half.at[pl.ds(k * part, part)]
        rest = pl.ds(0, edge) if k == 2 else pl.ds(edge + k * part, part)
        dst = density.at[rest, pl.ds(edge, edge)]
        return remote(src, dst, x_send.at[k], x_recv.at[k], "gx", row - 1)

    def keep(k):
        src = low if k == 2 else half.at[pl.ds(k * part, part)]
        rest = pl.ds(0, edge) if k == 2 else pl.ds(edge + k * part, part)
        return pltpu.make_async_copy(src, density.at[rest, pl.ds(0, edge)], own.at[2 + k])

    def start_y(k):
        @pl.when(me > 0)
        def _():
            along_y(k).start()

    def start_x(k):
        keep(k).start()

        @pl.when(row > 0)
        def _():
            along_x(k).start()

    def take_y(k):
        @pl.when(me < columns - 1)
        def _():
            along_y(k).wait_recv()

    for h in range(2):
        boxes_out.start(0, h)
    start_x(2)
    notes = [
        remote(table.at[target], places.at[me], table_send.at[k], table_recv.at[k], "gy", target)
        for k, target in enumerate(others)
    ]
    for note in notes:
        note.start()
    note = pltpu.make_async_copy(table.at[me], places.at[me], own.at[5])
    note.start()
    for h in range(2):
        boxes_out.forward(0, h)
    start_y(0)
    for h in range(2):
        boxes_out.arrive(0, h)
        boxes_out.start(1, h)
    take_y(0)
    start_x(0)
    for h in range(2):
        boxes_out.forward(1, h)
    start_y(1)
    for h in range(2):
        boxes_out.arrive(1, h)
    take_y(1)
    start_x(1)
    for k, sender in enumerate(senders):
        remote(
            table.at[me], places.at[sender], table_send.at[k], table_recv.at[k], "gy", sender
        ).wait_recv()
    for copy in notes:
        copy.wait_send()
    note.wait()
    for k in range(3):
        keep(k).wait()

        @pl.when(row > 0)
        def _():
            along_x(k).wait_send()

        @pl.when(row < rows - 1)
        def _():
            along_x(k).wait_recv()

    for k in range(2):

        @pl.when(me > 0)
        def _():
            along_y(k).wait_send()

    boxes_out.finish()


def rim_kernel(own, crowd, from_x, full, from_y, x_send, x_recv, y_send, y_recv):
    me, row = lax.axis_index("gy"), lax.axis_index("gx")
    columns, rows = lax.axis_size("gy"), lax.axis_size("gx")
    edge = own.shape[1] // 2
    part = edge // 2
    sides = (
        (row < rows - 1, row + 1, slice(edge, 2 * edge), 0),
        (row > 0, row - 1, slice(0, edge), 1),
    )
    count = 0
    for axis, at, size in (("gx", row, rows), ("gy", me, columns)):
        for there, target in ((at > 0, at - 1), (at < size - 1, at + 1)):
            count += there.astype(jnp.int32)

            @pl.when(there)
            def _():
                signal(axis, target)

    pl.semaphore_wait(pltpu.get_barrier_semaphore(), count)
    chunks = [slice(p, p + part) for p in (0, edge, part, edge + part)]

    def along_x(c, side):
        _, target, half, k = sides[side]
        return remote(
            own.at[chunks[c], half],
            from_x.at[k, chunks[c]],
            x_send.at[k, c],
            x_recv.at[k, c],
            "gx",
            target,
        )

    def along_y(c):
        start = chunks[c].start
        up = start >= edge
        target = me + 1 if up else me - 1
        rest = slice(start % edge, start % edge + part)
        copy = remote(
            full.at[chunks[c]], from_y.at[int(up), rest], y_send.at[c], y_recv.at[c], "gy", target
        )
        sends = me < columns - 1 if up else me > 0
        takes = me > 0 if up else me < columns - 1
        return copy, sends, takes

    for c in range(len(chunks)):
        for side in range(2):

            @pl.when(sides[side][0])
            def _():
                along_x(c, side).start()

    for c, rest in enumerate(chunks):
        for side in range(2):
            takes, half = sides[1 - side][0], slice(edge, 2 * edge) if side else slice(0, edge)

            @pl.when(takes)
            def _():
                along_x(c, side).wait_recv()
                full[rest, half] = own[rest, half] + from_x[side, rest]

            @pl.when(jnp.logical_not(takes))
            def _():
                full[rest, half] = own[rest, half]

        copy, sends, _ = along_y(c)

        @pl.when(sends)
        def _():
            copy.start()

    for c in range(len(chunks)):
        copy, sends, takes = along_y(c)
        up = chunks[c].start >= edge
        start = chunks[c].start % edge
        rest = slice(start, start + part)
        rows_in = slice(start, start + part) if up else slice(edge + start, edge + start + part)

        @pl.when(takes)
        def _():
            copy.wait_recv()
            crowd[rows_in] = full[rows_in].astype(jnp.float32) + from_y[int(up), rest].astype(jnp.float32)

        @pl.when(jnp.logical_not(takes))
        def _():
            crowd[rows_in] = full[rows_in].astype(jnp.float32)

        @pl.when(sends)
        def _():
            copy.wait_send()

        for side in range(2):

            @pl.when(sides[side][0])
            def _():
                along_x(c, side).wait_send()


def return_kernel(
    settled, wide, returned, deposit, stage, relay, from_x, outgoing, from_y,
    send, recv, x_send, x_recv, y_send, y_recv, own,
):
    me, row = lax.axis_index("gy"), lax.axis_index("gx")
    columns, rows = lax.axis_size("gy"), lax.axis_size("gx")
    edge = wide.shape[1] // 2
    count = greet()
    boxes_back = Exchange(settled, returned, stage, relay, send, recv, own, 1)
    boxes_back.prepare()
    pl.semaphore_wait(pltpu.get_barrier_semaphore(), count)
    halves = (slice(edge, 2 * edge), slice(0, edge))

    def along_x(k):
        return remote(
            wide.at[halves[k], pl.ds(edge, edge)], from_x.at[k], x_send.at[k], x_recv.at[k], "gx", row + 1
        )

    for h in range(2):
        boxes_back.start(0, h)

    @pl.when(row < rows - 1)
    def _():
        for k in range(2):
            along_x(k).start()

    for h in range(2):
        boxes_back.forward(0, h)

    @pl.when(row > 0)
    def _():
        along_x(0).wait_recv()
        outgoing[...] = wide[edge:, :edge] + from_x[0]

    @pl.when(row == 0)
    def _():
        outgoing[...] = wide[edge:, :edge]

    part = edge // 2

    def along_y(k):
        rest = pl.ds(k * part, part)
        return remote(
            outgoing.at[rest], from_y.at[rest], y_send.at[k], y_recv.at[k], "gy", me + 1
        )

    @pl.when(me < columns - 1)
    def _():
        along_y(0).start()

    for h in range(2):
        boxes_back.arrive(0, h)
        boxes_back.start(1, h)

    @pl.when(row > 0)
    def _():
        along_x(1).wait_recv()
        deposit[...] = wide[:edge, :edge].astype(jnp.float32) + from_x[1].astype(jnp.float32)

    @pl.when(row == 0)
    def _():
        deposit[...] = wide[:edge, :edge].astype(jnp.float32)

    for h in range(2):
        boxes_back.forward(1, h)

    @pl.when(me < columns - 1)
    def _():
        along_y(1).start()

    for h in range(2):
        boxes_back.arrive(1, h)

    @pl.when(me > 0)
    def _():
        for k in range(2):
            along_y(k).wait_recv()
        deposit[...] = deposit[...] + from_y[...].astype(jnp.float32)

    boxes_back.finish()

    @pl.when(me < columns - 1)
    def _():
        for k in range(2):
            along_y(k).wait_send()

    @pl.when(row < rows - 1)
    def _():
        for k in range(2):
            along_x(k).wait_send()


def fetch_places(table, places, sem):
    copy = pltpu.make_async_copy(table.at[:, 0], places, sem)
    copy.start()
    copy.wait()


def spread_base(base):
    row = lax.broadcasted_iota(jnp.int32, base.shape, 0)
    lane = lax.broadcasted_iota(jnp.int32, base.shape, 1)
    base[...] = jnp.where(row // LANES == lane // B, lax.rem(row, LANES) - lax.rem(lane, B), -1)


def stacked(boxes, s):
    return jnp.concatenate(
        [boxes[s, :, j * LANES : (j + 1) * LANES] for j in range(B // GROUP)], 0
    )


def add_box(wide, v, spread, lx, ly):
    placed = lax.dot_general(
        v, spread, (((1,), (1,)), ((), ())), preferred_element_type=jnp.float32
    )
    for j in range(B // GROUP):
        for i in range(GROUP):
            at = (ly + (GROUP * j + i), pl.ds(lx, B), slice(None))
            wide[at] = wide[at] + placed[j * B : (j + 1) * B, i * LANES : (i + 1) * LANES]


def take_box(field, spread, lx, ly):
    rows = []
    for j in range(B // GROUP):
        parts = [field[ly + (GROUP * j + i), pl.ds(lx, B), :] for i in range(GROUP)]
        rows.append(jnp.concatenate([p.astype(jnp.bfloat16) for p in parts], 1))
    return jnp.dot(jnp.concatenate(rows, 0), spread, preferred_element_type=jnp.float32)


def crowd_kernel(table, boxes, out, wide, base, places, sem):
    fetch_places(table, places, sem)
    wide[...] = jnp.zeros_like(wide)
    spread_base(base)

    def one(s, carry):
        @pl.when(places[s, 3] > 0)
        def _():
            lx, ly, lz = places[s, 0], places[s, 1], places[s, 2]
            spread = jnp.where(base[...] == lz, 1.0, 0.0).astype(jnp.bfloat16)
            v = stacked(boxes, s).astype(jnp.float32)
            add_box(wide, (v * v).astype(jnp.bfloat16), spread, lx, ly)

        return carry

    lax.fori_loop(0, boxes.shape[0], one, 0)
    out[...] = wide[...].astype(out.dtype)


def update_kernel(
    table, boxes, crowd, low, settled, out, density, wide, base, taps, places, sem
):
    fetch_places(table, places, sem)
    density[...] = low[...].astype(jnp.float32)
    wide[...] = jnp.zeros_like(wide)
    spread_base(base)
    from_b = lax.broadcasted_iota(jnp.int32, taps.shape, 0) - LANES
    to_b = lax.broadcasted_iota(jnp.int32, taps.shape, 1)
    gap = from_b - to_b
    beside = (gap == B) | (gap == -B)
    same = (from_b >= 0) & (from_b < LANES) & (lax.rem(from_b + LANES, LANES) // B == to_b // B)
    along = same & ((gap == 1) | (gap == -1))
    taps[...] = jnp.where(gap == 0, -6.0, jnp.where(beside | along, 1.0, 0.0)).astype(taps.dtype)
    step = lax.rem(lax.broadcasted_iota(jnp.int32, (B * B // GROUP, LANES), 0), B)
    edge = jnp.zeros((B, LANES), jnp.bfloat16)
    total = B * B // GROUP

    def one(s, carry):
        @pl.when(places[s, 3] > 0)
        def _():
            lx, ly, lz = places[s, 0], places[s, 1], places[s, 2]
            spread = jnp.where(base[...] == lz, 1.0, 0.0).astype(jnp.bfloat16)
            cr = take_box(crowd, spread, lx, ly)
            dn = take_box(density, spread, lx, ly)
            v = stacked(boxes, s)
            near = jnp.concatenate(
                [
                    jnp.concatenate([edge, v[: total - B]], 0),
                    v,
                    jnp.concatenate([v[B:], edge], 0),
                ],
                1,
            )
            lap = jnp.dot(near, taps[...], preferred_element_type=jnp.float32)
            p = v.astype(jnp.float32)
            across = jnp.where(step < B - 1, pltpu.roll(p, total - 1, 0), 0.0) + jnp.where(
                step > 0, pltpu.roll(p, 1, 0), 0.0
            )
            others = cr - p * p
            reaction = 4.0 * p * (1.0 - p) * (p - 0.5 + (dn - 0.5))
            fresh = p + 0.1 * (lap + across + reaction - 2.0 * p * others)
            fresh = fresh.astype(jnp.bfloat16)
            for j in range(B // GROUP):
                settled[s, :, j * LANES : (j + 1) * LANES] = fresh[j * B : (j + 1) * B]
            add_box(wide, fresh, spread, lx, ly)

        @pl.when(places[s, 3] <= 0)
        def _():
            settled[s] = jnp.zeros(settled.shape[1:], settled.dtype)

        return carry

    lax.fori_loop(0, boxes.shape[0], one, 0)
    out[...] = wide[...].astype(out.dtype)


VMEM = pl.BlockSpec(memory_space=pltpu.VMEM)
ANY = pl.BlockSpec(memory_space=pl.ANY)
SMEM = pl.BlockSpec(memory_space=pltpu.SMEM)
LIMIT = 24 * 2**20


def like(shape, dtype):
    return jax.ShapeDtypeStruct(shape, dtype)


def dma(*shape):
    return pltpu.SemaphoreType.DMA(shape)


def linked(number):
    return pltpu.CompilerParams(
        collective_id=number, has_side_effects=True, vmem_limit_bytes=LIMIT
    )


def per_device(phase_box, matrix_density, box_corner):
    slab_rows, slab_cols, grid_depth = matrix_density.shape
    peers = lax.axis_size("gy")
    cells = phase_box.shape[0]
    home = box_corner[1] // slab_cols
    local = jnp.stack(
        [
            box_corner[0] - lax.axis_index("gx") * slab_rows,
            box_corner[1] - home * slab_cols,
            box_corner[2],
            jnp.ones_like(home),
        ],
        1,
    )
    match = (home[None, :] == jnp.arange(peers, dtype=jnp.int32)[:, None]).astype(jnp.int32)
    source = jnp.sum(match * jnp.arange(cells, dtype=jnp.int32)[None, :], 1)
    table = jnp.sum(match[:, :, None] * local[None], 1)
    table = jnp.pad(jnp.broadcast_to(table[:, None], (peers, 8, 4)), ((0, 0), (0, 0), (0, LANES - 4)))
    low = jnp.swapaxes(matrix_density, 0, 1).astype(jnp.bfloat16)

    bf16, f32 = jnp.bfloat16, jnp.float32
    slots = (peers,) + phase_box.shape[1:]
    torus = (SIDE, SIDE) + phase_box.shape[1:]
    rows = (phase_box.shape[1] // 2,) + phase_box.shape[2:]
    moving = [pltpu.VMEM((2, SIDE, SIDE) + rows, bf16), pltpu.VMEM((2, 2, 2, SIDE - 1) + rows, bf16)]
    wide = (2 * slab_cols, 2 * slab_rows, grid_depth)
    half = (2 * slab_cols, slab_rows, grid_depth)
    quarter = (slab_cols, slab_rows, grid_depth)
    boxes, places, density = pl.pallas_call(
        gather_kernel,
        out_shape=(like(torus, bf16), like(table.shape, jnp.int32), like(wide, bf16)),
        in_specs=[SMEM, VMEM, VMEM, VMEM],
        out_specs=(ANY, ANY, ANY),
        scratch_shapes=[pltpu.VMEM(torus, bf16)]
        + moving
        + [
            pltpu.VMEM(quarter, bf16),
            dma(2, 2, 6), dma(2, 2, 6), dma(peers - 1), dma(peers - 1),
            dma(2), dma(2), dma(3), dma(3), dma(6),
        ],
        compiler_params=linked(0),
        name="gather",
    )(source, phase_box, table, low)
    boxes = boxes.reshape(slots)

    spread = pltpu.VMEM((GROUP * LANES, LANES), jnp.int32)
    taps = pltpu.VMEM((3 * LANES, LANES), bf16)
    spots = [pltpu.SMEM((peers, LANES), jnp.int32), dma()]
    quiet = pltpu.CompilerParams(vmem_limit_bytes=LIMIT)
    crowd = pl.pallas_call(
        crowd_kernel,
        out_shape=like(wide, bf16),
        in_specs=[ANY, VMEM],
        out_specs=VMEM,
        scratch_shapes=[pltpu.VMEM(wide, f32), spread] + spots,
        compiler_params=quiet,
        name="crowd",
    )(places, boxes)

    crowd = pl.pallas_call(
        rim_kernel,
        out_shape=like(wide, f32),
        in_specs=[VMEM],
        out_specs=VMEM,
        scratch_shapes=[
            pltpu.VMEM((2,) + half, bf16),
            pltpu.VMEM(wide, bf16),
            pltpu.VMEM((2, slab_cols) + wide[1:], bf16),
            dma(2, 4), dma(2, 4), dma(4), dma(4),
        ],
        compiler_params=linked(1),
        name="rim",
    )(crowd)

    settled, deposit = pl.pallas_call(
        update_kernel,
        out_shape=(like(slots, bf16), like(wide, bf16)),
        in_specs=[ANY, VMEM, VMEM, VMEM],
        out_specs=(VMEM, VMEM),
        scratch_shapes=[pltpu.VMEM(wide, f32), pltpu.VMEM(wide, f32), spread, taps] + spots,
        compiler_params=quiet,
        name="update",
    )(places, boxes, crowd, density)

    returned, deposit = pl.pallas_call(
        return_kernel,
        out_shape=(like(torus, bf16), like(quarter, f32)),
        in_specs=[VMEM, VMEM],
        out_specs=(ANY, VMEM),
        scratch_shapes=moving
        + [
            pltpu.VMEM((2,) + quarter, bf16),
            pltpu.VMEM(quarter, bf16),
            pltpu.VMEM(quarter, bf16),
            dma(2, 2, 6), dma(2, 2, 6), dma(2), dma(2), dma(2), dma(2), dma(2),
        ],
        compiler_params=linked(2),
        name="return",
    )(settled.reshape(torus), deposit)
    returned = returned.reshape(slots)

    phase_next = returned[home]
    matrix_next = matrix_density - 0.5 * matrix_density * jnp.swapaxes(deposit, 0, 1)
    return phase_next, matrix_next


def solution(mesh):
    return jax.shard_map(
        per_device,
        mesh=mesh,
        in_specs=(P(("gx", "gy"), None, None), P("gx", "gy", None), P(None, ("gx", "gy"))),
        out_specs=(P(("gx", "gy"), None, None), P("gx", "gy", None)),
        check_vma=False,
    )
```

profile of v0, /device:TPU:66, one launch (start us, length us, event | category | flops | bytes accessed | tf_op | source)
XLA Modules:
  0.0 94.0 jit_solution(9089457992536829774)
XLA Ops:
  0.6 0.8 subtract_bitcast_fusion
  1.4 0.7 fusion.3
  2.1 0.7 bitcast_subtract_fusion
  2.8 0.1 fusion.2
  2.9 0.1 multiply_reduce_fusion
  3.0 0.1 copy.15
  3.1 0.1 select_reduce_fusion.source
  3.2 1.4 %copy.24 = bf16[32,32,128]{2,0,1:T(8,128)(2,1)S(1)} copy(f32[32,32,128]{2,1,0:T(8,128)} %param.4) | data formatting | bytes 786432 | tf_op args[1]
  4.5 0.0 copy-start
  4.5 1.0 %copy-done = bf16[8,32,1024]{2,1,0:T(8,128)(2,1)S(1)} copy-done((bf16[8,32,1024]{2,1,0:T(8,128)(2,1)S(1)}, bf16[8,32,1024]{2,1,0:T(8,128)(2,1)}, u32[]{:S(2)}) %copy-start) | copy-done | bytes 524312
  5.6 26.9 %gather.7 = (bf16[4,4,32,1024]{3,2,1,0:T(8,128)(2,1)S(1)}, s32[16,8,128]{2,1,0:T(8,128)S(1)}, bf16[64,64,128]{2,1,0:T(8,128)(2,1)S(1)}) custom-call(s32[16]{0:T(128)S(1)} %select_reduce_fusion.source, bf16[8,32,1024]{2,1,0:T(8,128)(2,1)S(1)} %copy-done, s32[16,8,128]{2,1,0:T(8,128)S(1)} %pad.4.table, bf16[32,32,128]{2,1,0:T(8,128)(2,1)S(1)} %bitcast.30), custom_call_target="tpu_custom_call" | custom-call | tf_op jit(solution)/shard_map/gather/pallas_call | solution.py:631
  32.5 3.0 %crowd.1.own = bf16[64,64,128]{2,1,0:T(8,128)(2,1)S(1)} custom-call(s32[16,8,128]{2,1,0:T(8,128)S(1)} %get-tuple-element.9.table, bf16[16,32,1024]{2,1,0:T(8,128)(2,1)S(1)} %bitcast.28), custom_call_target="tpu_custom_call" | custom-call | tf_op jit(solution)/shard_map/crowd/pallas_call | solution.py:652
  35.5 23.8 %rim.1.crowd = f32[64,64,128]{2,1,0:T(8,128)S(1)} custom-call(bf16[64,64,128]{2,1,0:T(8,128)(2,1)S(1)} %crowd.1.own), custom_call_target="tpu_custom_call" | custom-call | tf_op jit(solution)/shard_map/rim/pallas_call | solution.py:662
  59.3 5.7 %update.1 = (bf16[16,32,1024]{2,1,0:T(8,128)(2,1)S(1)}, bf16[64,64,128]{2,1,0:T(8,128)(2,1)S(1)}) custom-call(s32[16,8,128]{2,1,0:T(8,128)S(1)} %get-tuple-element.9.table, bf16[16,32,1024]{2,1,0:T(8,128)(2,1)S(1)} %bitcast.29, f32[64,64,128]{2,1,0:T(8,128)S(1)} %rim.1.crowd, bf16[64,64,128]{2,1,0:T(8,128)(2,1)S(1)} %get-tuple-element.11.low), custom_call_target="tpu_custom_call" | custom-call | tf_op jit(solution)/shard_map/update/pallas_call | solution.py:677
  64.9 0.0 copy-start.1
  64.9 26.2 %return.1 = (bf16[4,4,32,1024]{3,2,1,0:T(8,128)(2,1)S(1)}, f32[32,32,128]{2,1,0:T(8,128)S(1)}) custom-call(bf16[4,4,32,1024]{3,2,1,0:T(8,128)(2,1)S(1)} %bitcast.31, bf16[64,64,128]{2,1,0:T(8,128)(2,1)S(1)} %get-tuple-element.13.wide), custom_call_target="tpu_custom_call" | custom-call | tf_op jit(solution)/shard_map/return/pallas_call | solution.py:687
  91.2 0.0 copy-done.1
  91.2 0.3 fusion
  91.5 1.1 %copy.19 = f32[32,32,128]{2,1,0:T(8,128)} copy(f32[32,32,128]{2,0,1:T(8,128)S(1)} %fusion) | data formatting | bytes 1048576
  92.6 1.4 %gather_fusion = bf16[8,32,1024]{2,1,0:T(8,128)(2,1)} fusion(bf16[16,32,1024]{2,1,0:T(8,128)(2,1)S(1)} %bitcast.32, s32[1024]{0:T(1024)S(1)} %pad_clamp_fusion), kind=kCustom, calls=%fused_computation | custom fusion | bytes 1048608 | tf_op jit(solution)/shard_map/gather | solution.py:704
  (5 shorter events, 0.0 us)
Async XLA Ops:
  4.5 1.0 %copy-start = (bf16[8,32,1024]{2,1,0:T(8,128)(2,1)S(1)}, bf16[8,32,1024]{2,1,0:T(8,128)(2,1)}, u32[]{:S(2)}) copy-start(bf16[8,32,1024]{2,1,0:T(8,128)(2,1)} %phase.1) | copy-start | bytes 1572868
  64.9 26.2 %copy-start.1 = (f32[32,32,128]{2,1,0:T(8,128)S(1)}, f32[32,32,128]{2,1,0:T(8,128)}, u32[]{:S(2)}) copy-start(f32[32,32,128]{2,1,0:T(8,128)} %param.4) | copy-start | bytes 1572868
where the time goes:
time: 95.2 us; the launch traced here: 94 us
  Pallas kernels  85.5 us (90%)
  local copies, waits for them, and re-layouts  4.97 us (5%)
  other arithmetic  2.79 us (3%)
    pallas_call x1, Pallas kernels, per_device(): pl.pallas_call(gather_kernel, out_shape=(like(torus, bf16), like(table.sh...  26.9 us
    pallas_call x1, Pallas kernels, per_device(): pl.pallas_call(return_kernel, out_shape=(like(torus, bf16), like(quarter,...  26.2 us
    pallas_call x1, Pallas kernels, per_device(): pl.pallas_call(rim_kernel, out_shape=like(wide, f32), in_specs=[VMEM], ou...  23.8 us
    pallas_call x1, Pallas kernels, per_device(): pl.pallas_call(update_kernel, out_shape=(like(slots, bf16), like(wide, bf...  5.68 us
    unnamed x6, local copies, waits for them, and re-layouts  3.49 us
    pallas_call x1, Pallas kernels, per_device(): pl.pallas_call(crowd_kernel, out_shape=like(wide, bf16), in_specs=[ANY, V...  2.99 us

commit v1 on v0

--- a/solution.py
+++ b/solution.py
@@ -156,13 +156,20 @@
 
 
 def gather_kernel(
-    source, phase, table, low, boxes, places, density,
-    outbox, stage, relay, half, send, recv, table_send, table_recv,
-    y_send, y_recv, x_send, x_recv, own,
+    corner_in, phase_in, density_in, boxes, places, density,
+    corner, phase, matrix, table, low, outbox, stage, relay, half, send, recv, table_send, table_recv,
+    y_send, y_recv, x_send, x_recv, own, fetch,
 ):
     me, row = lax.axis_index("gy"), lax.axis_index("gx")
     columns, rows = lax.axis_size("gy"), lax.axis_size("gx")
     edge = low.shape[0]
+    loads = [
+        pltpu.make_async_copy(phase_in, phase, fetch.at[0]),
+        pltpu.make_async_copy(density_in, matrix, fetch.at[1]),
+        pltpu.make_async_copy(corner_in, corner, fetch.at[2]),
+    ]
+    for load in loads:
+        load.start()
     part = edge // 2
     barrier = pltpu.get_barrier_semaphore()
     others = [lax.rem(me + k, columns) for k in range(1, columns)]
@@ -178,11 +185,33 @@
     def _():
         signal("gx", row + 1)
 
+    cells = range(phase.shape[0])
+    loads[2].wait()
+    home = [lax.div(corner[1, c], edge) for c in cells]
+    lane = lax.broadcasted_iota(jnp.int32, table.shape[1:], 1)
+    loads[0].wait()
+
     def fill(s, carry):
-        outbox[s // SIDE, lax.rem(s, SIDE)] = phase[source[s]]
+        source, found = jnp.int32(0), jnp.int32(0)
+        for c in cells:
+            source = jnp.where(home[c] == s, c, source)
+            found = jnp.where(home[c] == s, 1, found)
+        note = (
+            corner[0, source] - row * edge,
+            corner[1, source] - s * edge,
+            corner[2, source],
+            found,
+        )
+        line = jnp.zeros_like(lane)
+        for k, value in enumerate(note):
+            line = jnp.where(lane == k, value, line)
+        table[s] = line
+        outbox[s // SIDE, lax.rem(s, SIDE)] = phase[source]
         return carry
 
     lax.fori_loop(0, columns, fill, 0)
+    loads[1].wait()
+    low[...] = jnp.swapaxes(matrix[...], 0, 1).astype(low.dtype)
 
     @pl.when(me == columns - 1)
     def _():
@@ -240,6 +269,7 @@
     for h in range(2):
         boxes_out.forward(0, h)
     start_y(0)
+    start_y(1)
     for h in range(2):
         boxes_out.arrive(0, h)
         boxes_out.start(1, h)
@@ -247,11 +277,10 @@
     start_x(0)
     for h in range(2):
         boxes_out.forward(1, h)
-    start_y(1)
-    for h in range(2):
-        boxes_out.arrive(1, h)
     take_y(1)
     start_x(1)
+    for h in range(2):
+        boxes_out.arrive(1, h)
     for k, sender in enumerate(senders):
         remote(
             table.at[me], places.at[sender], table_send.at[k], table_recv.at[k], "gy", sender
@@ -424,7 +453,8 @@
 
     @pl.when(me < columns - 1)
     def _():
-        along_y(0).start()
+        for k in range(2):
+            along_y(k).start()
 
     for h in range(2):
         boxes_back.arrive(0, h)
@@ -441,19 +471,15 @@
 
     for h in range(2):
         boxes_back.forward(1, h)
-
-    @pl.when(me < columns - 1)
-    def _():
-        along_y(1).start()
-
-    for h in range(2):
-        boxes_back.arrive(1, h)
 
     @pl.when(me > 0)
     def _():
         for k in range(2):
             along_y(k).wait_recv()
         deposit[...] = deposit[...] + from_y[...].astype(jnp.float32)
+
+    for h in range(2):
+        boxes_back.arrive(1, h)
 
     boxes_back.finish()
 
@@ -580,9 +606,30 @@
     out[...] = wide[...].astype(out.dtype)
 
 
+def finish_kernel(
+    corner_in, returned, deposit, matrix, phase_next, matrix_next, corner, sem, fetch
+):
+    edge = matrix.shape[1]
+    load = pltpu.make_async_copy(corner_in, corner, fetch)
+    load.start()
+    load.wait()
+    copies = [
+        pltpu.make_async_copy(
+            returned.at[lax.div(corner[1, c], edge)], phase_next.at[c], sem.at[c]
+        )
+        for c in range(phase_next.shape[0])
+    ]
+    for copy in copies:
+        copy.start()
+    now = matrix[...]
+    matrix_next[...] = now - 0.5 * now * jnp.swapaxes(deposit[...], 0, 1)
+    for copy in copies:
+        copy.wait()
+
+
 VMEM = pl.BlockSpec(memory_space=pltpu.VMEM)
 ANY = pl.BlockSpec(memory_space=pl.ANY)
-SMEM = pl.BlockSpec(memory_space=pltpu.SMEM)
+HBM = pl.BlockSpec(memory_space=pltpu.HBM)
 LIMIT = 24 * 2**20
 
 
@@ -603,25 +650,9 @@
 def per_device(phase_box, matrix_density, box_corner):
     slab_rows, slab_cols, grid_depth = matrix_density.shape
     peers = lax.axis_size("gy")
-    cells = phase_box.shape[0]
-    home = box_corner[1] // slab_cols
-    local = jnp.stack(
-        [
-            box_corner[0] - lax.axis_index("gx") * slab_rows,
-            box_corner[1] - home * slab_cols,
-            box_corner[2],
-            jnp.ones_like(home),
-        ],
-        1,
-    )
-    match = (home[None, :] == jnp.arange(peers, dtype=jnp.int32)[:, None]).astype(jnp.int32)
-    source = jnp.sum(match * jnp.arange(cells, dtype=jnp.int32)[None, :], 1)
-    table = jnp.sum(match[:, :, None] * local[None], 1)
-    table = jnp.pad(jnp.broadcast_to(table[:, None], (peers, 8, 4)), ((0, 0), (0, 0), (0, LANES - 4)))
-    low = jnp.swapaxes(matrix_density, 0, 1).astype(jnp.bfloat16)
-
     bf16, f32 = jnp.bfloat16, jnp.float32
     slots = (peers,) + phase_box.shape[1:]
+    notes = (peers, 8, LANES)
     torus = (SIDE, SIDE) + phase_box.shape[1:]
     rows = (phase_box.shape[1] // 2,) + phase_box.shape[2:]
     moving = [pltpu.VMEM((2, SIDE, SIDE) + rows, bf16), pltpu.VMEM((2, 2, 2, SIDE - 1) + rows, bf16)]
@@ -630,19 +661,26 @@
     quarter = (slab_cols, slab_rows, grid_depth)
     boxes, places, density = pl.pallas_call(
         gather_kernel,
-        out_shape=(like(torus, bf16), like(table.shape, jnp.int32), like(wide, bf16)),
-        in_specs=[SMEM, VMEM, VMEM, VMEM],
+        out_shape=(like(torus, bf16), like(notes, jnp.int32), like(wide, bf16)),
+        in_specs=[HBM, HBM, HBM],
         out_specs=(ANY, ANY, ANY),
-        scratch_shapes=[pltpu.VMEM(torus, bf16)]
+        scratch_shapes=[
+            pltpu.SMEM(box_corner.shape, jnp.int32),
+            pltpu.VMEM(phase_box.shape, bf16),
+            pltpu.VMEM(matrix_density.shape, f32),
+            pltpu.VMEM(notes, jnp.int32),
+            pltpu.VMEM(quarter, bf16),
+            pltpu.VMEM(torus, bf16),
+        ]
         + moving
         + [
             pltpu.VMEM(quarter, bf16),
             dma(2, 2, 6), dma(2, 2, 6), dma(peers - 1), dma(peers - 1),
-            dma(2), dma(2), dma(3), dma(3), dma(6),
+            dma(2), dma(2), dma(3), dma(3), dma(6), dma(3),
         ],
         compiler_params=linked(0),
         name="gather",
-    )(source, phase_box, table, low)
+    )(box_corner, phase_box, matrix_density)
     boxes = boxes.reshape(slots)
 
     spread = pltpu.VMEM((GROUP * LANES, LANES), jnp.int32)
@@ -701,9 +739,19 @@
     )(settled.reshape(torus), deposit)
     returned = returned.reshape(slots)
 
-    phase_next = returned[home]
-    matrix_next = matrix_density - 0.5 * matrix_density * jnp.swapaxes(deposit, 0, 1)
-    return phase_next, matrix_next
+    return pl.pallas_call(
+        finish_kernel,
+        out_shape=(like(phase_box.shape, bf16), like(matrix_density.shape, f32)),
+        in_specs=[HBM, VMEM, VMEM, VMEM],
+        out_specs=(ANY, VMEM),
+        scratch_shapes=[
+            pltpu.SMEM(box_corner.shape, jnp.int32),
+            dma(phase_box.shape[0]),
+            dma(),
+        ],
+        compiler_params=quiet,
+        name="finish",
+    )(box_corner, returned, deposit, matrix_density)
 
 
 def solution(mesh):

time: 95.2 us -> 87.3 us (0.917)
  the two profiles are of different devices: /device:TPU:66 before, /device:TPU:64 now
where the time goes in v1:
time: 87.3 us; the launch traced here: 87.8 us
  Pallas kernels  84.4 us (97%)
  local copies, waits for them, and re-layouts  2.77 us (3%)
    pallas_call x1, Pallas kernels, per_device(): pl.pallas_call(return_kernel, out_shape=(like(torus, bf16), like(quarter,...  32 us
    pallas_call x1, Pallas kernels, per_device(): pl.pallas_call(gather_kernel, out_shape=(like(torus, bf16), like(notes, j...  25.3 us
    pallas_call x1, Pallas kernels, per_device(): pl.pallas_call(rim_kernel, out_shape=like(wide, f32), in_specs=[VMEM], ou...  19.8 us
    pallas_call x1, Pallas kernels, per_device(): pl.pallas_call(update_kernel, out_shape=(like(slots, bf16), like(wide, bf...  3.08 us
    unnamed x10, local copies, waits for them, and re-layouts  2.77 us
    pallas_call x1, Pallas kernels, per_device(): pl.pallas_call(finish_kernel, out_shape=(like(phase_box.shape, bf16), lik...  2.21 us
    pallas_call x1, Pallas kernels, per_device(): pl.pallas_call(crowd_kernel, out_shape=like(wide, bf16), in_specs=[ANY, V...  1.86 us

profile of v1, /device:TPU:64, one launch (start us, length us, event | category | flops | bytes accessed | tf_op | source)
XLA Modules:
  0.0 87.8 jit_solution(10333336053727851508)
XLA Ops:
  0.6 0.0 copy-start
  0.6 1.0 %copy-done = f32[32,32,128]{2,1,0:T(8,128)S(1)} copy-done((f32[32,32,128]{2,1,0:T(8,128)S(1)}, f32[32,32,128]{2,1,0:T(8,128)}, u32[]{:S(2)}) %copy-start) | copy-done | bytes 524312
  1.7 0.0 copy-start.2
  1.7 1.0 %copy-done.2 = bf16[8,32,1024]{2,1,0:T(8,128)(2,1)S(1)} copy-done((bf16[8,32,1024]{2,1,0:T(8,128)(2,1)S(1)}, bf16[8,32,1024]{2,1,0:T(8,128)(2,1)}, u32[]{:S(2)}) %copy-start.2) | copy-done | bytes 524312
  2.7 0.0 copy-start.3
  2.7 0.7 copy-done.3
  3.4 25.3 %gather.1 = (bf16[4,4,32,1024]{3,2,1,0:T(8,128)(2,1)S(1)}, s32[16,8,128]{2,1,0:T(8,128)S(1)}, bf16[64,64,128]{2,1,0:T(8,128)(2,1)S(1)}) custom-call(s32[3,8]{1,0:T(4,128)S(1)} %copy-done.3, bf16[8,32,1024]{2,1,0:T(8,128)(2,1)S(1)} %copy-done.2, f32[32,32,128]{2,1,0:T(8,128)S(1)} %copy-done), custom_call_target="tpu_custom_call" | custom-call | tf_op jit(solution)/shard_map/gather/pallas_call | solution.py:662
  28.7 1.9 %crowd.1.own = bf16[64,64,128]{2,1,0:T(8,128)(2,1)S(1)} custom-call(s32[16,8,128]{2,1,0:T(8,128)S(1)} %get-tuple-element.9.table, bf16[16,32,1024]{2,1,0:T(8,128)(2,1)S(1)} %bitcast.3), custom_call_target="tpu_custom_call" | custom-call | tf_op jit(solution)/shard_map/crowd/pallas_call | solution.py:690
  30.6 19.8 %rim.1.crowd = f32[64,64,128]{2,1,0:T(8,128)S(1)} custom-call(bf16[64,64,128]{2,1,0:T(8,128)(2,1)S(1)} %crowd.1.own), custom_call_target="tpu_custom_call" | custom-call | tf_op jit(solution)/shard_map/rim/pallas_call | solution.py:700
  50.5 3.1 %update.1 = (bf16[16,32,1024]{2,1,0:T(8,128)(2,1)S(1)}, bf16[64,64,128]{2,1,0:T(8,128)(2,1)S(1)}) custom-call(s32[16,8,128]{2,1,0:T(8,128)S(1)} %get-tuple-element.9.table, bf16[16,32,1024]{2,1,0:T(8,128)(2,1)S(1)} %bitcast.4, f32[64,64,128]{2,1,0:T(8,128)S(1)} %rim.1.crowd, bf16[64,64,128]{2,1,0:T(8,128)(2,1)S(1)} %get-tuple-element.11.low), custom_call_target="tpu_custom_call" | custom-call | tf_op jit(solution)/shard_map/update/pallas_call | solution.py:715
  53.5 0.0 copy-start.1
  53.5 0.0 copy-start.4
  53.6 32.0 %return.1 = (bf16[4,4,32,1024]{3,2,1,0:T(8,128)(2,1)S(1)}, f32[32,32,128]{2,1,0:T(8,128)S(1)}) custom-call(bf16[4,4,32,1024]{3,2,1,0:T(8,128)(2,1)S(1)} %bitcast.6, bf16[64,64,128]{2,1,0:T(8,128)(2,1)S(1)} %get-tuple-element.13.wide), custom_call_target="tpu_custom_call" | custom-call | tf_op jit(solution)/shard_map/return/pallas_call | solution.py:725
  85.6 0.0 copy-done.1
  85.6 0.0 copy-done.4
  85.6 2.2 %finish.1 = (bf16[8,32,1024]{2,1,0:T(8,128)(2,1)}, f32[32,32,128]{2,1,0:T(8,128)}) custom-call(s32[3,8]{1,0:T(4,128)S(1)} %copy-done.4, bf16[16,32,1024]{2,1,0:T(8,128)(2,1)S(1)} %bitcast.5, f32[32,32,128]{2,1,0:T(8,128)S(1)} %get-tuple-element.15.deposit, f32[32,32,128]{2,1,0:T(8,128)S(1)} %copy-done.1), custom_call_target="tpu_custom_call" | custom-call | tf_op jit(solution)/shard_map/finish/pallas_call | solution.py:742
Async XLA Ops:
  0.6 1.0 %copy-start = (f32[32,32,128]{2,1,0:T(8,128)S(1)}, f32[32,32,128]{2,1,0:T(8,128)}, u32[]{:S(2)}) copy-start(f32[32,32,128]{2,1,0:T(8,128)} %matrix.1) | copy-start | bytes 1572868
  1.7 1.0 %copy-start.2 = (bf16[8,32,1024]{2,1,0:T(8,128)(2,1)S(1)}, bf16[8,32,1024]{2,1,0:T(8,128)(2,1)}, u32[]{:S(2)}) copy-start(bf16[8,32,1024]{2,1,0:T(8,128)(2,1)} %phase_in.1) | copy-start | bytes 1572868
  2.7 0.7 copy-start.3
  53.5 32.1 %copy-start.1 = (f32[32,32,128]{2,1,0:T(8,128)S(1)}, f32[32,32,128]{2,1,0:T(8,128)}, u32[]{:S(2)}) copy-start(f32[32,32,128]{2,1,0:T(8,128)} %matrix.1) | copy-start | bytes 1572868
  53.5 32.1 %copy-start.4 = (s32[3,8]{1,0:T(4,128)S(1)}, s32[3,8]{1,0:T(4,128)}, u32[]{:S(2)}) copy-start(s32[3,8]{1,0:T(4,128)} %corner_in.3) | copy-start | bytes 292

commit v2 on v1

--- a/solution.py
+++ b/solution.py
@@ -607,11 +607,15 @@
 
 
 def finish_kernel(
-    corner_in, returned, deposit, matrix, phase_next, matrix_next, corner, sem, fetch
+    corner_in, returned, deposit, matrix, phase_next, matrix_next, corner, turned, sem, fetch
 ):
     edge = matrix.shape[1]
-    load = pltpu.make_async_copy(corner_in, corner, fetch)
+    load = pltpu.make_async_copy(corner_in, corner, fetch.at[0])
     load.start()
+    now = matrix[...]
+    turned[...] = now - 0.5 * now * jnp.swapaxes(deposit[...], 0, 1)
+    store = pltpu.make_async_copy(turned, matrix_next, fetch.at[1])
+    store.start()
     load.wait()
     copies = [
         pltpu.make_async_copy(
@@ -621,8 +625,7 @@
     ]
     for copy in copies:
         copy.start()
-    now = matrix[...]
-    matrix_next[...] = now - 0.5 * now * jnp.swapaxes(deposit[...], 0, 1)
+    store.wait()
     for copy in copies:
         copy.wait()
 
@@ -680,7 +683,9 @@
         ],
         compiler_params=linked(0),
         name="gather",
-    )(box_corner, phase_box, matrix_density)
+    )(
+        *(pltpu.with_memory_space_constraint(a, pltpu.HBM) for a in (box_corner, phase_box, matrix_density))
+    )
     boxes = boxes.reshape(slots)
 
     spread = pltpu.VMEM((GROUP * LANES, LANES), jnp.int32)
@@ -743,15 +748,18 @@
         finish_kernel,
         out_shape=(like(phase_box.shape, bf16), like(matrix_density.shape, f32)),
         in_specs=[HBM, VMEM, VMEM, VMEM],
-        out_specs=(ANY, VMEM),
+        out_specs=(ANY, ANY),
         scratch_shapes=[
             pltpu.SMEM(box_corner.shape, jnp.int32),
+            pltpu.VMEM(matrix_density.shape, f32),
             dma(phase_box.shape[0]),
-            dma(),
+            dma(2),
         ],
         compiler_params=quiet,
         name="finish",
-    )(box_corner, returned, deposit, matrix_density)
+    )(
+        pltpu.with_memory_space_constraint(box_corner, pltpu.HBM), returned, deposit, matrix_density
+    )
 
 
 def solution(mesh):

time: 87.3 us -> 83.8 us (0.960)
  local copies, waits for them, and re-layouts: 2.77 us -> 0.01 us
  Pallas kernels: 84.4 us -> 83 us
    unnamed x10 -> x2, local copies, waits for them, and re-layouts: 2.77 us -> 0.01 us
    pallas_call x1, Pallas kernels: 32 us -> 30.3 us  [per_device(): pl.pallas_call(return_kernel, out_shape=(like(torus, bf16), like(quarter,...]
    pallas_call x1, Pallas kernels: 3.08 us -> 4.1 us  [per_device(): pl.pallas_call(update_kernel, out_shape=(like(slots, bf16), like(wide, bf...]
where the time goes in v2:
time: 83.8 us; the launch traced here: 83.7 us
  Pallas kernels  83 us (99%)
    pallas_call x1, Pallas kernels, per_device(): pl.pallas_call(return_kernel, out_shape=(like(torus, bf16), like(quarter,...  30.3 us
    pallas_call x1, Pallas kernels, per_device(): pl.pallas_call(gather_kernel, out_shape=(like(torus, bf16), like(notes, j...  25.3 us
    pallas_call x1, Pallas kernels, per_device(): pl.pallas_call(rim_kernel, out_shape=like(wide, f32), in_specs=[VMEM], ou...  19.3 us
    pallas_call x1, Pallas kernels, per_device(): pl.pallas_call(update_kernel, out_shape=(like(slots, bf16), like(wide, bf...  4.1 us
    pallas_call x1, Pallas kernels, per_device(): pl.pallas_call(crowd_kernel, out_shape=like(wide, bf16), in_specs=[ANY, V...  2.33 us

profile of v2, /device:TPU:64, one launch (start us, length us, event | category | flops | bytes accessed | tf_op | source)
XLA Modules:
  0.0 83.7 jit_solution(16618931516218296150)
XLA Ops:
  0.6 25.3 %gather.1 = (bf16[4,4,32,1024]{3,2,1,0:T(8,128)(2,1)S(1)}, s32[16,8,128]{2,1,0:T(8,128)S(1)}, bf16[64,64,128]{2,1,0:T(8,128)(2,1)S(1)}) custom-call(s32[3,8]{1,0:T(4,128)} %corner_in.3, bf16[8,32,1024]{2,1,0:T(8,128)(2,1)} %phase_in.1, f32[32,32,128]{2,1,0:T(8,128)} %matrix.1), custom_call_target="tpu_custom_call" | custom-call | tf_op jit(solution)/shard_map/gather/pallas_call | solution.py:665
  26.0 2.3 %crowd.1.own = bf16[64,64,128]{2,1,0:T(8,128)(2,1)S(1)} custom-call(s32[16,8,128]{2,1,0:T(8,128)S(1)} %get-tuple-element.9.table, bf16[16,32,1024]{2,1,0:T(8,128)(2,1)S(1)} %bitcast.3), custom_call_target="tpu_custom_call" | custom-call | tf_op jit(solution)/shard_map/crowd/pallas_call | solution.py:695
  28.3 19.3 %rim.1.crowd = f32[64,64,128]{2,1,0:T(8,128)S(1)} custom-call(bf16[64,64,128]{2,1,0:T(8,128)(2,1)S(1)} %crowd.1.own), custom_call_target="tpu_custom_call" | custom-call | tf_op jit(solution)/shard_map/rim/pallas_call | solution.py:705
  47.7 4.1 %update.1 = (bf16[16,32,1024]{2,1,0:T(8,128)(2,1)S(1)}, bf16[64,64,128]{2,1,0:T(8,128)(2,1)S(1)}) custom-call(s32[16,8,128]{2,1,0:T(8,128)S(1)} %get-tuple-element.9.table, bf16[16,32,1024]{2,1,0:T(8,128)(2,1)S(1)} %bitcast.4, f32[64,64,128]{2,1,0:T(8,128)S(1)} %rim.1.crowd, bf16[64,64,128]{2,1,0:T(8,128)(2,1)S(1)} %get-tuple-element.11.low), custom_call_target="tpu_custom_call" | custom-call | tf_op jit(solution)/shard_map/update/pallas_call | solution.py:720
  51.8 0.0 copy-start
  51.8 30.3 %return.1 = (bf16[4,4,32,1024]{3,2,1,0:T(8,128)(2,1)S(1)}, f32[32,32,128]{2,1,0:T(8,128)S(1)}) custom-call(bf16[4,4,32,1024]{3,2,1,0:T(8,128)(2,1)S(1)} %bitcast.6, bf16[64,64,128]{2,1,0:T(8,128)(2,1)S(1)} %get-tuple-element.13.wide), custom_call_target="tpu_custom_call" | custom-call | tf_op jit(solution)/shard_map/return/pallas_call | solution.py:730
  82.1 0.0 copy-done
  82.1 1.6 %finish.1 = (bf16[8,32,1024]{2,1,0:T(8,128)(2,1)}, f32[32,32,128]{2,1,0:T(8,128)}) custom-call(s32[3,8]{1,0:T(4,128)} %corner_in.3, bf16[16,32,1024]{2,1,0:T(8,128)(2,1)S(1)} %bitcast.5, f32[32,32,128]{2,1,0:T(8,128)S(1)} %get-tuple-element.15.deposit, f32[32,32,128]{2,1,0:T(8,128)S(1)} %copy-done), custom_call_target="tpu_custom_call" | custom-call | tf_op jit(solution)/shard_map/finish/pallas_call | solution.py:747
Async XLA Ops:
  51.8 30.4 %copy-start = (f32[32,32,128]{2,1,0:T(8,128)S(1)}, f32[32,32,128]{2,1,0:T(8,128)}, u32[]{:S(2)}) copy-start(f32[32,32,128]{2,1,0:T(8,128)} %matrix.1) | copy-start | bytes 1572868

commit v3 on v2

--- a/solution.py
+++ b/solution.py
@@ -9,6 +9,7 @@
 LANES = 128
 GROUP = LANES // B
 SIDE = 4
+RIM_CHUNKS = 4
 
 def signal(axis, target):
     pl.semaphore_signal(
@@ -308,15 +309,14 @@
     boxes_out.finish()
 
 
-def rim_kernel(own, crowd, from_x, full, from_y, x_send, x_recv, y_send, y_recv):
+def rim_kernel(
+    own, crowd, from_x, full, from_y, done, back,
+    x_send, x_recv, y_send, y_recv, b_send, b_recv,
+):
     me, row = lax.axis_index("gy"), lax.axis_index("gx")
     columns, rows = lax.axis_size("gy"), lax.axis_size("gx")
     edge = own.shape[1] // 2
-    part = edge // 2
-    sides = (
-        (row < rows - 1, row + 1, slice(edge, 2 * edge), 0),
-        (row > 0, row - 1, slice(0, edge), 1),
-    )
+    chunks, _, part, _ = full.shape
     count = 0
     for axis, at, size in (("gx", row, rows), ("gy", me, columns)):
         for there, target in ((at > 0, at - 1), (at < size - 1, at + 1)):
@@ -327,82 +327,89 @@
                 signal(axis, target)
 
     pl.semaphore_wait(pltpu.get_barrier_semaphore(), count)
-    chunks = [slice(p, p + part) for p in (0, edge, part, edge + part)]
-
-    def along_x(c, side):
-        _, target, half, k = sides[side]
+    low, high = slice(0, edge), slice(edge, 2 * edge)
+    ups = ((me < columns - 1, me > 0, me + 1, high, low), (me > 0, me < columns - 1, me - 1, low, high))
+
+    def spill(c):
+        src = own.at[:, pl.ds(edge + c * part, part)]
+        return remote(src, from_x.at[c], x_send.at[c], x_recv.at[c], "gx", row + 1)
+
+    def exchange(c, k):
+        _, _, target, sent, _ = ups[k]
         return remote(
-            own.at[chunks[c], half],
-            from_x.at[k, chunks[c]],
-            x_send.at[k, c],
-            x_recv.at[k, c],
-            "gx",
-            target,
+            full.at[c, sent], from_y.at[k, c], y_send.at[k, c], y_recv.at[k, c], "gy", target
         )
 
-    def along_y(c):
-        start = chunks[c].start
-        up = start >= edge
-        target = me + 1 if up else me - 1
-        rest = slice(start % edge, start % edge + part)
-        copy = remote(
-            full.at[chunks[c]], from_y.at[int(up), rest], y_send.at[c], y_recv.at[c], "gy", target
-        )
-        sends = me < columns - 1 if up else me > 0
-        takes = me > 0 if up else me < columns - 1
-        return copy, sends, takes
-
-    for c in range(len(chunks)):
-        for side in range(2):
-
-            @pl.when(sides[side][0])
+    def give(c):
+        return remote(done.at[c], back.at[c], b_send.at[c], b_recv.at[c], "gx", row - 1)
+
+    @pl.when(row < rows - 1)
+    def _():
+        for c in range(chunks):
+            spill(c).start()
+
+    for c in range(chunks):
+        mine = slice(c * part, (c + 1) * part)
+
+        @pl.when(row > 0)
+        def _():
+            spill(c).wait_recv()
+            full[c] = own[:, mine] + from_x[c]
+
+        @pl.when(row == 0)
+        def _():
+            full[c] = own[:, mine]
+
+        for k in range(2):
+
+            @pl.when(ups[k][0])
             def _():
-                along_x(c, side).start()
-
-    for c, rest in enumerate(chunks):
-        for side in range(2):
-            takes, half = sides[1 - side][0], slice(edge, 2 * edge) if side else slice(0, edge)
+                exchange(c, k).start()
+
+    for c in range(chunks):
+        for k in range(2):
+            _, takes, _, _, into = ups[k]
 
             @pl.when(takes)
             def _():
-                along_x(c, side).wait_recv()
-                full[rest, half] = own[rest, half] + from_x[side, rest]
+                exchange(c, k).wait_recv()
+                done[c, into] = full[c, into] + from_y[k, c]
 
             @pl.when(jnp.logical_not(takes))
             def _():
-                full[rest, half] = own[rest, half]
-
-        copy, sends, _ = along_y(c)
-
-        @pl.when(sends)
-        def _():
-            copy.start()
-
-    for c in range(len(chunks)):
-        copy, sends, takes = along_y(c)
-        up = chunks[c].start >= edge
-        start = chunks[c].start % edge
-        rest = slice(start, start + part)
-        rows_in = slice(start, start + part) if up else slice(edge + start, edge + start + part)
-
-        @pl.when(takes)
-        def _():
-            copy.wait_recv()
-            crowd[rows_in] = full[rows_in].astype(jnp.float32) + from_y[int(up), rest].astype(jnp.float32)
-
-        @pl.when(jnp.logical_not(takes))
-        def _():
-            crowd[rows_in] = full[rows_in].astype(jnp.float32)
-
-        @pl.when(sends)
-        def _():
-            copy.wait_send()
-
-        for side in range(2):
-
-            @pl.when(sides[side][0])
+                done[c, into] = full[c, into]
+
+        @pl.when(row > 0)
+        def _():
+            give(c).start()
+
+        crowd[:, c * part : (c + 1) * part] = done[c].astype(jnp.float32)
+
+    @pl.when(row == rows - 1)
+    def _():
+        crowd[:, edge:] = jnp.zeros((crowd.shape[0], edge, crowd.shape[2]), jnp.float32)
+
+    @pl.when(row < rows - 1)
+    def _():
+        for c in range(chunks):
+            give(c).wait_recv()
+            crowd[:, edge + c * part : edge + (c + 1) * part] = back[c].astype(jnp.float32)
+
+    for c in range(chunks):
+
+        @pl.when(row < rows - 1)
+        def _():
+            spill(c).wait_send()
+
+        for k in range(2):
+
+            @pl.when(ups[k][0])
             def _():
-                along_x(c, side).wait_send()
+                exchange(c, k).wait_send()
+
+        @pl.when(row > 0)
+        def _():
+            give(c).wait_send()
 
 
 def return_kernel(
@@ -660,7 +667,7 @@
     rows = (phase_box.shape[1] // 2,) + phase_box.shape[2:]
     moving = [pltpu.VMEM((2, SIDE, SIDE) + rows, bf16), pltpu.VMEM((2, 2, 2, SIDE - 1) + rows, bf16)]
     wide = (2 * slab_cols, 2 * slab_rows, grid_depth)
-    half = (2 * slab_cols, slab_rows, grid_depth)
+    strips = (RIM_CHUNKS, 2 * slab_cols, slab_rows // RIM_CHUNKS, grid_depth)
     quarter = (slab_cols, slab_rows, grid_depth)
     boxes, places, density = pl.pallas_call(
         gather_kernel,
@@ -708,10 +715,13 @@
         in_specs=[VMEM],
         out_specs=VMEM,
         scratch_shapes=[
-            pltpu.VMEM((2,) + half, bf16),
-            pltpu.VMEM(wide, bf16),
-            pltpu.VMEM((2, slab_cols) + wide[1:], bf16),
-            dma(2, 4), dma(2, 4), dma(4), dma(4),
+            pltpu.VMEM(strips, bf16),
+            pltpu.VMEM(strips, bf16),
+            pltpu.VMEM((2, RIM_CHUNKS, slab_cols) + strips[2:], bf16),
+            pltpu.VMEM(strips, bf16),
+            pltpu.VMEM(strips, bf16),
+            dma(RIM_CHUNKS), dma(RIM_CHUNKS), dma(2, RIM_CHUNKS), dma(2, RIM_CHUNKS),
+            dma(RIM_CHUNKS), dma(RIM_CHUNKS),
         ],
         compiler_params=linked(1),
         name="rim",

time: 83.8 us -> 82.6 us (0.986); the launches traced: 83.7 us -> 81.4 us
  Pallas kernels: 83 us -> 80.7 us
    pallas_call x1, Pallas kernels: 30.3 us -> 23.4 us  [per_device(): pl.pallas_call(return_kernel, out_shape=(like(torus, bf16), like(quarter,...]
    pallas_call x1, Pallas kernels: 4.1 us -> 9.86 us  [per_device(): pl.pallas_call(update_kernel, out_shape=(like(slots, bf16), like(wide, bf...]
    pallas_call x1, Pallas kernels: 19.3 us -> 15.8 us  [per_device(): pl.pallas_call(rim_kernel, out_shape=like(wide, f32), in_specs=[VMEM], ou...]
    pallas_call x1, Pallas kernels: 2.33 us -> 4.85 us  [per_device(): pl.pallas_call(crowd_kernel, out_shape=like(wide, bf16), in_specs=[ANY, V...]
where the time goes in v3:
time: 82.6 us; the launch traced here: 81.4 us
  Pallas kernels  80.7 us (98%)
    pallas_call x1, Pallas kernels, per_device(): pl.pallas_call(gather_kernel, out_shape=(like(torus, bf16), like(notes, j...  25.3 us
    pallas_call x1, Pallas kernels, per_device(): pl.pallas_call(return_kernel, out_shape=(like(torus, bf16), like(quarter,...  23.4 us
    pallas_call x1, Pallas kernels, per_device(): pl.pallas_call(rim_kernel, out_shape=like(wide, f32), in_specs=[VMEM], ou...  15.8 us
    pallas_call x1, Pallas kernels, per_device(): pl.pallas_call(update_kernel, out_shape=(like(slots, bf16), like(wide, bf...  9.86 us
    pallas_call x1, Pallas kernels, per_device(): pl.pallas_call(crowd_kernel, out_shape=like(wide, bf16), in_specs=[ANY, V...  4.85 us

profile of v3, /device:TPU:64, one launch (start us, length us, event | category | flops | bytes accessed | tf_op | source)
XLA Modules:
  0.0 81.4 jit_solution(8806363846721167859)
XLA Ops:
  0.6 25.3 %gather.1 = (bf16[4,4,32,1024]{3,2,1,0:T(8,128)(2,1)S(1)}, s32[16,8,128]{2,1,0:T(8,128)S(1)}, bf16[64,64,128]{2,1,0:T(8,128)(2,1)S(1)}) custom-call(s32[3,8]{1,0:T(4,128)} %corner_in.3, bf16[8,32,1024]{2,1,0:T(8,128)(2,1)} %phase_in.1, f32[32,32,128]{2,1,0:T(8,128)} %matrix.1), custom_call_target="tpu_custom_call" | custom-call | tf_op jit(solution)/shard_map/gather/pallas_call | solution.py:672
  26.0 4.9 %crowd.1.own = bf16[64,64,128]{2,1,0:T(8,128)(2,1)S(1)} custom-call(s32[16,8,128]{2,1,0:T(8,128)S(1)} %get-tuple-element.9.table, bf16[16,32,1024]{2,1,0:T(8,128)(2,1)S(1)} %bitcast.3), custom_call_target="tpu_custom_call" | custom-call | tf_op jit(solution)/shard_map/crowd/pallas_call | solution.py:702
  30.8 15.8 %rim.1.crowd = f32[64,64,128]{2,1,0:T(8,128)S(1)} custom-call(bf16[64,64,128]{2,1,0:T(8,128)(2,1)S(1)} %crowd.1.own), custom_call_target="tpu_custom_call" | custom-call | tf_op jit(solution)/shard_map/rim/pallas_call | solution.py:712
  46.6 9.9 %update.1 = (bf16[16,32,1024]{2,1,0:T(8,128)(2,1)S(1)}, bf16[64,64,128]{2,1,0:T(8,128)(2,1)S(1)}) custom-call(s32[16,8,128]{2,1,0:T(8,128)S(1)} %get-tuple-element.9.table, bf16[16,32,1024]{2,1,0:T(8,128)(2,1)S(1)} %bitcast.4, f32[64,64,128]{2,1,0:T(8,128)S(1)} %rim.1.crowd, bf16[64,64,128]{2,1,0:T(8,128)(2,1)S(1)} %get-tuple-element.11.low), custom_call_target="tpu_custom_call" | custom-call | tf_op jit(solution)/shard_map/update/pallas_call | solution.py:730
  56.5 0.0 copy-start
  56.5 23.4 %return.1 = (bf16[4,4,32,1024]{3,2,1,0:T(8,128)(2,1)S(1)}, f32[32,32,128]{2,1,0:T(8,128)S(1)}) custom-call(bf16[4,4,32,1024]{3,2,1,0:T(8,128)(2,1)S(1)} %bitcast.6, bf16[64,64,128]{2,1,0:T(8,128)(2,1)S(1)} %get-tuple-element.13.wide), custom_call_target="tpu_custom_call" | custom-call | tf_op jit(solution)/shard_map/return/pallas_call | solution.py:740
  79.9 0.0 copy-done
  79.9 1.6 %finish.1 = (bf16[8,32,1024]{2,1,0:T(8,128)(2,1)}, f32[32,32,128]{2,1,0:T(8,128)}) custom-call(s32[3,8]{1,0:T(4,128)} %corner_in.3, bf16[16,32,1024]{2,1,0:T(8,128)(2,1)S(1)} %bitcast.5, f32[32,32,128]{2,1,0:T(8,128)S(1)} %get-tuple-element.15.deposit, f32[32,32,128]{2,1,0:T(8,128)S(1)} %copy-done), custom_call_target="tpu_custom_call" | custom-call | tf_op jit(solution)/shard_map/finish/pallas_call | solution.py:757
Async XLA Ops:
  56.5 23.4 %copy-start = (f32[32,32,128]{2,1,0:T(8,128)S(1)}, f32[32,32,128]{2,1,0:T(8,128)}, u32[]{:S(2)}) copy-start(f32[32,32,128]{2,1,0:T(8,128)} %matrix.1) | copy-start | bytes 1572868

commit v4 on v3

--- a/solution.py
+++ b/solution.py
@@ -9,6 +9,7 @@
 LANES = 128
 GROUP = LANES // B
 SIDE = 4
+TOGETHER = 2
 RIM_CHUNKS = 4
 
 def signal(axis, target):
@@ -199,7 +200,7 @@
             found = jnp.where(home[c] == s, 1, found)
         note = (
             corner[0, source] - row * edge,
-            corner[1, source] - s * edge,
+            jnp.where(found > 0, corner[1, source] - s * edge, 0),
             corner[2, source],
             found,
         )
@@ -513,10 +514,11 @@
     base[...] = jnp.where(row // LANES == lane // B, lax.rem(row, LANES) - lax.rem(lane, B), -1)
 
 
-def stacked(boxes, s):
-    return jnp.concatenate(
+def stacked(boxes, s, here):
+    v = jnp.concatenate(
         [boxes[s, :, j * LANES : (j + 1) * LANES] for j in range(B // GROUP)], 0
     )
+    return jnp.where(here, v, jnp.zeros_like(v))
 
 
 def add_box(wide, v, spread, lx, ly):
@@ -542,17 +544,22 @@
     wide[...] = jnp.zeros_like(wide)
     spread_base(base)
 
-    def one(s, carry):
-        @pl.when(places[s, 3] > 0)
-        def _():
-            lx, ly, lz = places[s, 0], places[s, 1], places[s, 2]
-            spread = jnp.where(base[...] == lz, 1.0, 0.0).astype(jnp.bfloat16)
-            v = stacked(boxes, s).astype(jnp.float32)
-            add_box(wide, (v * v).astype(jnp.bfloat16), spread, lx, ly)
+    def one(t, carry):
+        slots = [t * TOGETHER + k for k in range(TOGETHER)]
+
+        @pl.when(sum(places[s, 3] for s in slots) > 0)
+        def _():
+            squares, spreads = [], []
+            for s in slots:
+                v = stacked(boxes, s, places[s, 3] > 0).astype(jnp.float32)
+                squares.append((v * v).astype(jnp.bfloat16))
+                spreads.append(jnp.where(base[...] == places[s, 2], 1.0, 0.0).astype(jnp.bfloat16))
+            for s, square, spread in zip(slots, squares, spreads):
+                add_box(wide, square, spread, places[s, 0], places[s, 1])
 
         return carry
 
-    lax.fori_loop(0, boxes.shape[0], one, 0)
+    lax.fori_loop(0, boxes.shape[0] // TOGETHER, one, 0)
     out[...] = wide[...].astype(out.dtype)
 
 
@@ -574,42 +581,51 @@
     edge = jnp.zeros((B, LANES), jnp.bfloat16)
     total = B * B // GROUP
 
-    def one(s, carry):
-        @pl.when(places[s, 3] > 0)
-        def _():
-            lx, ly, lz = places[s, 0], places[s, 1], places[s, 2]
-            spread = jnp.where(base[...] == lz, 1.0, 0.0).astype(jnp.bfloat16)
-            cr = take_box(crowd, spread, lx, ly)
-            dn = take_box(density, spread, lx, ly)
-            v = stacked(boxes, s)
-            near = jnp.concatenate(
-                [
-                    jnp.concatenate([edge, v[: total - B]], 0),
-                    v,
-                    jnp.concatenate([v[B:], edge], 0),
-                ],
-                1,
-            )
-            lap = jnp.dot(near, taps[...], preferred_element_type=jnp.float32)
-            p = v.astype(jnp.float32)
-            across = jnp.where(step < B - 1, pltpu.roll(p, total - 1, 0), 0.0) + jnp.where(
-                step > 0, pltpu.roll(p, 1, 0), 0.0
-            )
-            others = cr - p * p
-            reaction = 4.0 * p * (1.0 - p) * (p - 0.5 + (dn - 0.5))
-            fresh = p + 0.1 * (lap + across + reaction - 2.0 * p * others)
-            fresh = fresh.astype(jnp.bfloat16)
-            for j in range(B // GROUP):
-                settled[s, :, j * LANES : (j + 1) * LANES] = fresh[j * B : (j + 1) * B]
-            add_box(wide, fresh, spread, lx, ly)
-
-        @pl.when(places[s, 3] <= 0)
-        def _():
-            settled[s] = jnp.zeros(settled.shape[1:], settled.dtype)
+    def one(t, carry):
+        slots = [t * TOGETHER + k for k in range(TOGETHER)]
+        busy = sum(places[s, 3] for s in slots) > 0
+
+        @pl.when(busy)
+        def _():
+            spreads, results = [], []
+            for s in slots:
+                lx, ly, lz = places[s, 0], places[s, 1], places[s, 2]
+                spread = jnp.where(base[...] == lz, 1.0, 0.0).astype(jnp.bfloat16)
+                cr = take_box(crowd, spread, lx, ly)
+                dn = take_box(density, spread, lx, ly)
+                v = stacked(boxes, s, places[s, 3] > 0)
+                near = jnp.concatenate(
+                    [
+                        jnp.concatenate([edge, v[: total - B]], 0),
+                        v,
+                        jnp.concatenate([v[B:], edge], 0),
+                    ],
+                    1,
+                )
+                lap = jnp.dot(near, taps[...], preferred_element_type=jnp.float32)
+                p = v.astype(jnp.float32)
+                across = jnp.where(step < B - 1, pltpu.roll(p, total - 1, 0), 0.0) + jnp.where(
+                    step > 0, pltpu.roll(p, 1, 0), 0.0
+                )
+                others = cr - p * p
+                reaction = 4.0 * p * (1.0 - p) * (p - 0.5 + (dn - 0.5))
+                fresh = p + 0.1 * (lap + across + reaction - 2.0 * p * others)
+                fresh = fresh.astype(jnp.bfloat16)
+                for j in range(B // GROUP):
+                    settled[s, :, j * LANES : (j + 1) * LANES] = fresh[j * B : (j + 1) * B]
+                spreads.append(spread)
+                results.append(fresh)
+            for s, fresh, spread in zip(slots, results, spreads):
+                add_box(wide, fresh, spread, places[s, 0], places[s, 1])
+
+        @pl.when(jnp.logical_not(busy))
+        def _():
+            for s in slots:
+                settled[s] = jnp.zeros(settled.shape[1:], settled.dtype)
 
         return carry
 
-    lax.fori_loop(0, boxes.shape[0], one, 0)
+    lax.fori_loop(0, boxes.shape[0] // TOGETHER, one, 0)
     out[...] = wide[...].astype(out.dtype)
 
 

time: 82.6 us -> 78.5 us (0.950)
  Pallas kernels: 80.7 us -> 77.4 us
    pallas_call x1, Pallas kernels: 9.86 us -> 7.42 us  [per_device(): pl.pallas_call(update_kernel, out_shape=(like(slots, bf16), like(wide, bf...]
    pallas_call x1, Pallas kernels: 4.85 us -> 3.65 us  [per_device(): pl.pallas_call(crowd_kernel, out_shape=like(wide, bf16), in_specs=[ANY, V...]
where the time goes in v4:
time: 78.5 us; the launch traced here: 78 us
  Pallas kernels  77.4 us (99%)
    pallas_call x1, Pallas kernels, per_device(): pl.pallas_call(gather_kernel, out_shape=(like(torus, bf16), like(notes, j...  25.3 us
    pallas_call x1, Pallas kernels, per_device(): pl.pallas_call(return_kernel, out_shape=(like(torus, bf16), like(quarter,...  23.6 us
    pallas_call x1, Pallas kernels, per_device(): pl.pallas_call(rim_kernel, out_shape=like(wide, f32), in_specs=[VMEM], ou...  15.8 us
    pallas_call x1, Pallas kernels, per_device(): pl.pallas_call(update_kernel, out_shape=(like(slots, bf16), like(wide, bf...  7.42 us
    pallas_call x1, Pallas kernels, per_device(): pl.pallas_call(crowd_kernel, out_shape=like(wide, bf16), in_specs=[ANY, V...  3.65 us

profile of v4, /device:TPU:64, one launch (start us, length us, event | category | flops | bytes accessed | tf_op | source)
XLA Modules:
  0.0 78.0 jit_solution(14950533117139216888)
XLA Ops:
  0.6 25.3 %gather.1 = (bf16[4,4,32,1024]{3,2,1,0:T(8,128)(2,1)S(1)}, s32[16,8,128]{2,1,0:T(8,128)S(1)}, bf16[64,64,128]{2,1,0:T(8,128)(2,1)S(1)}) custom-call(s32[3,8]{1,0:T(4,128)} %corner_in.3, bf16[8,32,1024]{2,1,0:T(8,128)(2,1)} %phase_in.1, f32[32,32,128]{2,1,0:T(8,128)} %matrix.1), custom_call_target="tpu_custom_call" | custom-call | tf_op jit(solution)/shard_map/gather/pallas_call | solution.py:688
  26.0 3.7 %crowd.1.own = bf16[64,64,128]{2,1,0:T(8,128)(2,1)S(1)} custom-call(s32[16,8,128]{2,1,0:T(8,128)S(1)} %get-tuple-element.9.table, bf16[16,32,1024]{2,1,0:T(8,128)(2,1)S(1)} %bitcast.3), custom_call_target="tpu_custom_call" | custom-call | tf_op jit(solution)/shard_map/crowd/pallas_call | solution.py:718
  29.6 15.8 %rim.1.crowd = f32[64,64,128]{2,1,0:T(8,128)S(1)} custom-call(bf16[64,64,128]{2,1,0:T(8,128)(2,1)S(1)} %crowd.1.own), custom_call_target="tpu_custom_call" | custom-call | tf_op jit(solution)/shard_map/rim/pallas_call | solution.py:728
  45.4 7.4 %update.1 = (bf16[16,32,1024]{2,1,0:T(8,128)(2,1)S(1)}, bf16[64,64,128]{2,1,0:T(8,128)(2,1)S(1)}) custom-call(s32[16,8,128]{2,1,0:T(8,128)S(1)} %get-tuple-element.9.table, bf16[16,32,1024]{2,1,0:T(8,128)(2,1)S(1)} %bitcast.4, f32[64,64,128]{2,1,0:T(8,128)S(1)} %rim.1.crowd, bf16[64,64,128]{2,1,0:T(8,128)(2,1)S(1)} %get-tuple-element.11.low), custom_call_target="tpu_custom_call" | custom-call | tf_op jit(solution)/shard_map/update/pallas_call | solution.py:746
  52.8 0.0 copy-start
  52.8 23.6 %return.1 = (bf16[4,4,32,1024]{3,2,1,0:T(8,128)(2,1)S(1)}, f32[32,32,128]{2,1,0:T(8,128)S(1)}) custom-call(bf16[4,4,32,1024]{3,2,1,0:T(8,128)(2,1)S(1)} %bitcast.6, bf16[64,64,128]{2,1,0:T(8,128)(2,1)S(1)} %get-tuple-element.13.wide), custom_call_target="tpu_custom_call" | custom-call | tf_op jit(solution)/shard_map/return/pallas_call | solution.py:756
  76.5 0.0 copy-done
  76.5 1.6 %finish.1 = (bf16[8,32,1024]{2,1,0:T(8,128)(2,1)}, f32[32,32,128]{2,1,0:T(8,128)}) custom-call(s32[3,8]{1,0:T(4,128)} %corner_in.3, bf16[16,32,1024]{2,1,0:T(8,128)(2,1)S(1)} %bitcast.5, f32[32,32,128]{2,1,0:T(8,128)S(1)} %get-tuple-element.15.deposit, f32[32,32,128]{2,1,0:T(8,128)S(1)} %copy-done), custom_call_target="tpu_custom_call" | custom-call | tf_op jit(solution)/shard_map/finish/pallas_call | solution.py:773
Async XLA Ops:
  52.8 23.7 %copy-start = (f32[32,32,128]{2,1,0:T(8,128)S(1)}, f32[32,32,128]{2,1,0:T(8,128)}, u32[]{:S(2)}) copy-start(f32[32,32,128]{2,1,0:T(8,128)} %matrix.1) | copy-start | bytes 1572868

commit v5 on v4

--- a/solution.py
+++ b/solution.py
@@ -9,7 +9,7 @@
 LANES = 128
 GROUP = LANES // B
 SIDE = 4
-TOGETHER = 2
+TOGETHER = 4
 RIM_CHUNKS = 4
 
 def signal(axis, target):

time: 78.5 us -> 77 us (0.981)
  Pallas kernels: 77.4 us -> 75.8 us
    pallas_call x1, Pallas kernels: 3.65 us -> 2.83 us  [per_device(): pl.pallas_call(crowd_kernel, out_shape=like(wide, bf16), in_specs=[ANY, V...]
where the time goes in v5:
time: 77 us; the launch traced here: 76.5 us
  Pallas kernels  75.8 us (98%)
    pallas_call x1, Pallas kernels, per_device(): pl.pallas_call(gather_kernel, out_shape=(like(torus, bf16), like(notes, j...  25.3 us
    pallas_call x1, Pallas kernels, per_device(): pl.pallas_call(return_kernel, out_shape=(like(torus, bf16), like(quarter,...  23.6 us
    pallas_call x1, Pallas kernels, per_device(): pl.pallas_call(rim_kernel, out_shape=like(wide, f32), in_specs=[VMEM], ou...  15.8 us
    pallas_call x1, Pallas kernels, per_device(): pl.pallas_call(update_kernel, out_shape=(like(slots, bf16), like(wide, bf...  6.72 us
    pallas_call x1, Pallas kernels, per_device(): pl.pallas_call(crowd_kernel, out_shape=like(wide, bf16), in_specs=[ANY, V...  2.83 us
    pallas_call x1, Pallas kernels, per_device(): pl.pallas_call(finish_kernel, out_shape=(like(phase_box.shape, bf16), lik...  1.56 us

profile of v5, /device:TPU:64, one launch (start us, length us, event | category | flops | bytes accessed | tf_op | source)
XLA Modules:
  0.0 76.5 jit_solution(1986549744408350838)
XLA Ops:
  0.6 25.3 %gather.1 = (bf16[4,4,32,1024]{3,2,1,0:T(8,128)(2,1)S(1)}, s32[16,8,128]{2,1,0:T(8,128)S(1)}, bf16[64,64,128]{2,1,0:T(8,128)(2,1)S(1)}) custom-call(s32[3,8]{1,0:T(4,128)} %corner_in.3, bf16[8,32,1024]{2,1,0:T(8,128)(2,1)} %phase_in.1, f32[32,32,128]{2,1,0:T(8,128)} %matrix.1), custom_call_target="tpu_custom_call" | custom-call | tf_op jit(solution)/shard_map/gather/pallas_call | solution.py:688
  26.0 2.8 %crowd.1.own = bf16[64,64,128]{2,1,0:T(8,128)(2,1)S(1)} custom-call(s32[16,8,128]{2,1,0:T(8,128)S(1)} %get-tuple-element.9.table, bf16[16,32,1024]{2,1,0:T(8,128)(2,1)S(1)} %bitcast.3), custom_call_target="tpu_custom_call" | custom-call | tf_op jit(solution)/shard_map/crowd/pallas_call | solution.py:718
  28.8 15.8 %rim.1.crowd = f32[64,64,128]{2,1,0:T(8,128)S(1)} custom-call(bf16[64,64,128]{2,1,0:T(8,128)(2,1)S(1)} %crowd.1.own), custom_call_target="tpu_custom_call" | custom-call | tf_op jit(solution)/shard_map/rim/pallas_call | solution.py:728
  44.6 6.7 %update.1 = (bf16[16,32,1024]{2,1,0:T(8,128)(2,1)S(1)}, bf16[64,64,128]{2,1,0:T(8,128)(2,1)S(1)}) custom-call(s32[16,8,128]{2,1,0:T(8,128)S(1)} %get-tuple-element.9.table, bf16[16,32,1024]{2,1,0:T(8,128)(2,1)S(1)} %bitcast.4, f32[64,64,128]{2,1,0:T(8,128)S(1)} %rim.1.crowd, bf16[64,64,128]{2,1,0:T(8,128)(2,1)S(1)} %get-tuple-element.11.low), custom_call_target="tpu_custom_call" | custom-call | tf_op jit(solution)/shard_map/update/pallas_call | solution.py:746
  51.3 0.0 copy-start
  51.3 23.6 %return.1 = (bf16[4,4,32,1024]{3,2,1,0:T(8,128)(2,1)S(1)}, f32[32,32,128]{2,1,0:T(8,128)S(1)}) custom-call(bf16[4,4,32,1024]{3,2,1,0:T(8,128)(2,1)S(1)} %bitcast.6, bf16[64,64,128]{2,1,0:T(8,128)(2,1)S(1)} %get-tuple-element.13.wide), custom_call_target="tpu_custom_call" | custom-call | tf_op jit(solution)/shard_map/return/pallas_call | solution.py:756
  74.9 0.0 copy-done
  75.0 1.6 %finish.1 = (bf16[8,32,1024]{2,1,0:T(8,128)(2,1)}, f32[32,32,128]{2,1,0:T(8,128)}) custom-call(s32[3,8]{1,0:T(4,128)} %corner_in.3, bf16[16,32,1024]{2,1,0:T(8,128)(2,1)S(1)} %bitcast.5, f32[32,32,128]{2,1,0:T(8,128)S(1)} %get-tuple-element.15.deposit, f32[32,32,128]{2,1,0:T(8,128)S(1)} %copy-done), custom_call_target="tpu_custom_call" | custom-call | tf_op jit(solution)/shard_map/finish/pallas_call | solution.py:773
Async XLA Ops:
  51.3 23.7 %copy-start = (f32[32,32,128]{2,1,0:T(8,128)S(1)}, f32[32,32,128]{2,1,0:T(8,128)}, u32[]{:S(2)}) copy-start(f32[32,32,128]{2,1,0:T(8,128)} %matrix.1) | copy-start | bytes 1572868

commit v6 on v5

--- a/solution.py
+++ b/solution.py
@@ -9,7 +9,7 @@
 LANES = 128
 GROUP = LANES // B
 SIDE = 4
-TOGETHER = 4
+TOGETHER = 8
 RIM_CHUNKS = 4
 
 def signal(axis, target):

time: 77 us -> 76.8 us (level)
  no operation moved by 1% of the time
where the time goes in v6:
time: 76.8 us; the launch traced here: 76.1 us
  Pallas kernels  75.4 us (98%)
    pallas_call x1, Pallas kernels, per_device(): pl.pallas_call(gather_kernel, out_shape=(like(torus, bf16), like(notes, j...  25.3 us
    pallas_call x1, Pallas kernels, per_device(): pl.pallas_call(return_kernel, out_shape=(like(torus, bf16), like(quarter,...  23.6 us
    pallas_call x1, Pallas kernels, per_device(): pl.pallas_call(rim_kernel, out_shape=like(wide, f32), in_specs=[VMEM], ou...  15.8 us
    pallas_call x1, Pallas kernels, per_device(): pl.pallas_call(update_kernel, out_shape=(like(slots, bf16), like(wide, bf...  6.53 us
    pallas_call x1, Pallas kernels, per_device(): pl.pallas_call(crowd_kernel, out_shape=like(wide, bf16), in_specs=[ANY, V...  2.55 us
    pallas_call x1, Pallas kernels, per_device(): pl.pallas_call(finish_kernel, out_shape=(like(phase_box.shape, bf16), lik...  1.56 us

profile of v6, /device:TPU:64, one launch (start us, length us, event | category | flops | bytes accessed | tf_op | source)
XLA Modules:
  0.0 76.1 jit_solution(6905390323498640753)
XLA Ops:
  0.6 25.3 %gather.1 = (bf16[4,4,32,1024]{3,2,1,0:T(8,128)(2,1)S(1)}, s32[16,8,128]{2,1,0:T(8,128)S(1)}, bf16[64,64,128]{2,1,0:T(8,128)(2,1)S(1)}) custom-call(s32[3,8]{1,0:T(4,128)} %corner_in.3, bf16[8,32,1024]{2,1,0:T(8,128)(2,1)} %phase_in.1, f32[32,32,128]{2,1,0:T(8,128)} %matrix.1), custom_call_target="tpu_custom_call" | custom-call | tf_op jit(solution)/shard_map/gather/pallas_call | solution.py:688
  26.0 2.5 %crowd.1.own = bf16[64,64,128]{2,1,0:T(8,128)(2,1)S(1)} custom-call(s32[16,8,128]{2,1,0:T(8,128)S(1)} %get-tuple-element.9.table, bf16[16,32,1024]{2,1,0:T(8,128)(2,1)S(1)} %bitcast.3), custom_call_target="tpu_custom_call" | custom-call | tf_op jit(solution)/shard_map/crowd/pallas_call | solution.py:718
  28.5 15.8 %rim.1.crowd = f32[64,64,128]{2,1,0:T(8,128)S(1)} custom-call(bf16[64,64,128]{2,1,0:T(8,128)(2,1)S(1)} %crowd.1.own), custom_call_target="tpu_custom_call" | custom-call | tf_op jit(solution)/shard_map/rim/pallas_call | solution.py:728
  44.3 6.5 %update.1 = (bf16[16,32,1024]{2,1,0:T(8,128)(2,1)S(1)}, bf16[64,64,128]{2,1,0:T(8,128)(2,1)S(1)}) custom-call(s32[16,8,128]{2,1,0:T(8,128)S(1)} %get-tuple-element.9.table, bf16[16,32,1024]{2,1,0:T(8,128)(2,1)S(1)} %bitcast.4, f32[64,64,128]{2,1,0:T(8,128)S(1)} %rim.1.crowd, bf16[64,64,128]{2,1,0:T(8,128)(2,1)S(1)} %get-tuple-element.11.low), custom_call_target="tpu_custom_call" | custom-call | tf_op jit(solution)/shard_map/update/pallas_call | solution.py:746
  50.8 0.0 copy-start
  50.8 23.6 %return.1 = (bf16[4,4,32,1024]{3,2,1,0:T(8,128)(2,1)S(1)}, f32[32,32,128]{2,1,0:T(8,128)S(1)}) custom-call(bf16[4,4,32,1024]{3,2,1,0:T(8,128)(2,1)S(1)} %bitcast.6, bf16[64,64,128]{2,1,0:T(8,128)(2,1)S(1)} %get-tuple-element.13.wide), custom_call_target="tpu_custom_call" | custom-call | tf_op jit(solution)/shard_map/return/pallas_call | solution.py:756
  74.5 0.0 copy-done
  74.5 1.6 %finish.1 = (bf16[8,32,1024]{2,1,0:T(8,128)(2,1)}, f32[32,32,128]{2,1,0:T(8,128)}) custom-call(s32[3,8]{1,0:T(4,128)} %corner_in.3, bf16[16,32,1024]{2,1,0:T(8,128)(2,1)S(1)} %bitcast.5, f32[32,32,128]{2,1,0:T(8,128)S(1)} %get-tuple-element.15.deposit, f32[32,32,128]{2,1,0:T(8,128)S(1)} %copy-done), custom_call_target="tpu_custom_call" | custom-call | tf_op jit(solution)/shard_map/finish/pallas_call | solution.py:773
Async XLA Ops:
  50.8 23.6 %copy-start = (f32[32,32,128]{2,1,0:T(8,128)S(1)}, f32[32,32,128]{2,1,0:T(8,128)}, u32[]{:S(2)}) copy-start(f32[32,32,128]{2,1,0:T(8,128)} %matrix.1) | copy-start | bytes 1572868
